TPU v7x, 32 devices: a whole 2x2x4 slice. The times are simulated.
32 devices in a mesh: gx: 4 (over y, x), gy: 2 (over core), gz: 4 (over z).
Axes of the slice: x: 2, y: 2, z: 4, core: 2. Of those that a mesh axis runs over, the one named last changes fastest.
Arguments:
- right_side: float32 [8, 32, 64, 512], P(None, 'gx', 'gy', 'gz'), may hold values from -12 to 12
- shift: float32 [32, 64, 512], P('gx', 'gy', 'gz'), may hold values from 0.02 to 2
Outputs:
- solution_block: float32 [8, 32, 64, 512], P(None, 'gx', 'gy', 'gz')
- residual_norms: float32 [8], replicated
All inputs are finite; a program needn't handle non-finite values.
Results may differ from a plain program's by a relative error of at most 0.0003.
Values sent between devices are 32-bit elements; how exact they have to be, the bound alone decides.
No kernel may reach another device: no remote copies, remote signals or barrier semaphores. Data moves between devices by JAX's collectives and lax.ppermute only.
A program may use at most 128 MiB of HBM per device.

v0:
```python
import jax
import jax.numpy as jnp
from jax import lax
from jax.sharding import PartitionSpec as P

ITERS = 2


def padded_2(block, sides, width):
    for axis, dim in sides:
        count = lax.axis_size(axis)
        forward = [(i, i + 1) for i in range(count - 1)]
        backward = [(target, source) for source, target in forward]
        low = lax.ppermute(
            lax.slice_in_dim(block, block.shape[dim] - width, None, axis=dim), axis, forward
        )
        high = lax.ppermute(lax.slice_in_dim(block, 0, width, axis=dim), axis, backward)
        block = jnp.concatenate([low, block, high], axis=dim)
    return block


def operate(fields, shift):
    padded = padded_2(fields, (("gx", 1), ("gy", 2), ("gz", 3)), 1)
    beside = padded[:, 2:, 1:-1, 1:-1] + padded[:, :-2, 1:-1, 1:-1]
    beside = beside + padded[:, 1:-1, 2:, 1:-1] + padded[:, 1:-1, :-2, 1:-1]
    beside = beside + padded[:, 1:-1, 1:-1, 2:] + padded[:, 1:-1, 1:-1, :-2]
    return (6.0 + shift)[None] * fields - beside


def lower_inverse(lower):
    count = lower.shape[0]
    return jax.scipy.linalg.solve_triangular(lower, jnp.eye(count, dtype=lower.dtype), lower=True)


def small_dot(left, right):
    return jnp.dot(left, right, precision=lax.Precision.HIGHEST)


def body(right_side, shift):
    width = right_side.shape[0]
    shape = right_side.shape
    rows = right_side.reshape(width, -1)
    gram = lax.psum(small_dot(rows, rows.T), ("gx", "gy", "gz"))
    lower = jnp.linalg.cholesky(gram)
    start_coeff = lower.T
    basis = [small_dot(lower_inverse(lower), rows)]
    hessen = jnp.zeros(((ITERS + 1) * width, ITERS * width), jnp.float32)
    for step in range(ITERS):
        image = operate(basis[step].reshape(shape), shift).reshape(width, -1)
        stacked = jnp.concatenate(basis, axis=0)
        products = lax.psum(
            small_dot(jnp.concatenate([stacked, image], axis=0), image.T), ("gx", "gy", "gz")
        )
        coeffs = products[:-width]
        gram = products[-width:] - small_dot(coeffs.T, coeffs)
        projected = image - small_dot(coeffs.T, stacked)
        lower = jnp.linalg.cholesky(gram)
        hessen = hessen.at[: (step + 1) * width, step * width : (step + 1) * width].set(coeffs)
        hessen = hessen.at[
            (step + 1) * width : (step + 2) * width, step * width : (step + 1) * width
        ].set(lower.T)
        if step + 1 < ITERS:
            basis.append(small_dot(lower_inverse(lower), projected))
    target = jnp.zeros(((ITERS + 1) * width, width), jnp.float32).at[:width].set(start_coeff)
    normal = small_dot(hessen.T, hessen)
    factor = jnp.linalg.cholesky(normal)
    coeff_y = jax.scipy.linalg.cho_solve((factor, True), small_dot(hessen.T, target))
    solution = small_dot(coeff_y.T, jnp.concatenate(basis, axis=0)).reshape(shape)
    leftover = target - small_dot(hessen, coeff_y)
    norms = jnp.sqrt(jnp.sum(leftover * leftover, axis=0))
    return (solution, norms)


def solution(mesh):
    in_specs = (P(None, "gx", "gy", "gz"), P("gx", "gy", "gz"))
    out_specs = (P(None, "gx", "gy", "gz"), P())
    return jax.shard_map(body, mesh=mesh, in_specs=in_specs, out_specs=out_specs, check_vma=False)
```

profile of v0, /device:TPU:0, one launch (start us, length us, event | category | flops | bytes accessed | tf_op | source)
XLA Modules:
  0.0 228.1 jit_solution(12695287434098205644)
XLA Ops:
  0.6 4.9 %convolution_bitcast_fusion = f32[8,8]{0,1:T(8,128)S(1)} fusion(f32[8,8,32,128]{3,2,1,0:T(8,128)} %param.15), kind=kOutput, calls=%fused_computation.19 | convolution fusion | flops 25165824 | bytes 1048832 | tf_op jit(solution)/shard_map/dot_general | solution.py:36
  5.5 42.0 %psum.21 = f32[8,8]{0,1:T(8,128)S(1)} all-reduce(f32[8,8]{0,1:T(8,128)S(1)} %convolution_bitcast_fusion), channel_id=1, replica_groups=mesh['gx'=4,'gy'=2,'gz'=4] {'gx','gy','gz'}, use_global_device_ids=true, to_apply=%region_0.0 | all-reduce | flops 64 | bytes 512 | tf_op jit(solution)/shard_map/psum | solution.py:43
  47.5 0.7 cholesky.94
  50.4 1.5 fusion.12
  51.9 1.3 collective-permute-start
  53.2 4.8 %collective-permute-start.1 = (f32[8,1,32,128]{3,0,2,1:T(8,128)S(1)}, f32[8,1,32,128]{3,0,2,1:T(8,128)S(1)}, u32[]{:S(2)}, u32[]{:S(2)}) collective-permute-start(f32[8,1,32,128]{3,0,2,1:T(8,128)S(1)} %get-tuple-element.84), channel_id=1, source_target_pairs={{0,8},{8,16},{16,24},{1,9},{9,17},{17,25},{2,10},{10,18},{18,26},{... | collective-permute-start | bytes 393224 | tf_op jit(solution)/shard_map/ppermute | solution.py:14
  58.1 1.0 collective-permute-done
  59.1 1.5 collective-permute-done.1
  60.6 1.3 collective-permute-start.2
  61.9 3.0 %collective-permute-start.3 = (f32[8,10,1,128]{3,0,2,1:T(8,128)S(1)}, f32[8,10,1,128]{3,0,2,1:T(8,128)S(1)}, u32[]{:S(2)}, u32[]{:S(2)}) collective-permute-start(f32[8,10,1,128]{3,0,2,1:T(8,128)S(1)} %get-tuple-element.80), channel_id=1, source_target_pairs={{0,4},{1,5},{2,6},{3,7},{8,12},{9,13},{10,14},{11,15},{16,20},{17,... | collective-permute-start | bytes 122888 | tf_op jit(solution)/shard_map/ppermute | solution.py:14
  64.9 0.8 collective-permute-done.3
  66.4 1.5 fusion.56
  67.9 2.0 copy.130
  70.0 1.3 collective-permute-start.4
  71.2 0.7 copy.132
  71.9 4.5 %collective-permute-start.5 = (f32[8,10,34,1]{2,0,3,1:T(8,128)S(1)}, f32[8,10,34,1]{2,0,3,1:T(8,128)S(1)}, u32[]{:S(2)}, u32[]{:S(2)}) collective-permute-start(f32[8,10,34,1]{2,0,3,1:T(8,128)S(1)} %copy.132), channel_id=1, source_target_pairs={{0,1},{1,2},{2,3},{4,5},{5,6},{6,7},{8,9},{9,10},{10,11},{12,13},{... | collective-permute-start | bytes 32648 | tf_op jit(solution)/shard_map/ppermute | solution.py:14
  77.1 0.7 copy.131
  78.1 1.8 copy.133
  79.9 3.0 %fusion.22 = f32[8,8,32,128]{3,0,2,1:T(8,128)S(1)} fusion(f32[8,10,34,1]{3,0,2,1:T(8,128)} %copy.133, f32[8,10,1,128]{3,0,2,1:T(8,128)S(1)} %collective-permute-done.2, f32[8,10,1,128]{3,0,2,1:T(8,128)} %copy-done.6, f32[8,1,32,128]{3,0,2,1:T(8,128)} %copy-done.3, f32[8,8,32,128]{3,0,2,1:T(8,128)S(1)} %bitcast.73, f32[8,1,32,128]{3,0,2,1:T(8,128)} %copy-done.4, ...), kind=kLoop, calls=%fused_computation.50 | loop fusion | flops 6553600 | bytes 2594048 | tf_op jit(solution)/shard_map/sub | solution.py:27
  82.9 2.6 %fusion.6 = f32[16,8]{0,1:T(8,128)S(1)} fusion(f32[8,32768]{1,0:T(8,128)S(1)} %bitcast.78, f32[8,32768]{1,0:T(8,128)S(1)} %fusion.12), kind=kOutput, calls=%fused_computation.9 | convolution fusion | flops 50855936 | bytes 2097664 | tf_op jit(solution)/shard_map/dot_general | solution.py:36
  85.5 43.2 %psum.22 = f32[16,8]{0,1:T(8,128)S(1)} all-reduce(f32[16,8]{0,1:T(8,128)S(1)} %fusion.6), channel_id=1, replica_groups=mesh['gx'=4,'gy'=2,'gz'=4] {'gx','gy','gz'}, use_global_device_ids=true, to_apply=%region_3.0 | all-reduce | flops 128 | bytes 1024 | tf_op jit(solution)/shard_map/psum | solution.py:51
  128.6 1.0 convolution_subtract_fusion
  129.8 0.7 cholesky.105
  132.7 1.0 fusion.60
  133.7 1.3 collective-permute-start.6
  135.0 4.8 %collective-permute-start.7 = (f32[8,1,32,128]{3,0,2,1:T(8,128)S(1)}, f32[8,1,32,128]{3,0,2,1:T(8,128)S(1)}, u32[]{:S(2)}, u32[]{:S(2)}) collective-permute-start(f32[8,1,32,128]{3,0,2,1:T(8,128)S(1)} %get-tuple-element.82), channel_id=1, source_target_pairs={{0,8},{8,16},{16,24},{1,9},{9,17},{17,25},{2,10},{10,18},{18,26},{... | collective-permute-start | bytes 393224 | tf_op jit(solution)/shard_map/ppermute | solution.py:14
  139.9 1.2 collective-permute-done.6
  141.1 1.3 collective-permute-done.7
  142.4 1.3 collective-permute-start.8
  143.7 3.0 %collective-permute-start.9 = (f32[8,10,1,128]{3,0,2,1:T(8,128)S(1)}, f32[8,10,1,128]{3,0,2,1:T(8,128)S(1)}, u32[]{:S(2)}, u32[]{:S(2)}) collective-permute-start(f32[8,10,1,128]{3,0,2,1:T(8,128)S(1)} %get-tuple-element.78), channel_id=1, source_target_pairs={{0,4},{1,5},{2,6},{3,7},{8,12},{9,13},{10,14},{11,15},{16,20},{17,... | collective-permute-start | bytes 122888 | tf_op jit(solution)/shard_map/ppermute | solution.py:14
  146.7 0.8 collective-permute-done.9
  148.3 1.5 fusion.55
  149.8 2.6 %copy.137 = f32[8,10,34,1]{2,0,3,1:T(8,128)} copy(f32[8,10,34,1]{3,0,2,1:T(8,128)} %get-tuple-element.74) | data formatting | bytes 21760 | tf_op jit(solution)/shard_map/slice | solution.py:17
  152.4 1.3 collective-permute-start.10
  153.7 1.3 copy.139
  155.0 5.2 %collective-permute-start.11 = (f32[8,10,34,1]{2,0,3,1:T(8,128)}, f32[8,10,34,1]{2,0,3,1:T(8,128)}, u32[]{:S(2)}, u32[]{:S(2)}) collective-permute-start(f32[8,10,34,1]{2,0,3,1:T(8,128)} %copy.139), channel_id=1, source_target_pairs={{0,1},{1,2},{2,3},{4,5},{5,6},{6,7},{8,9},{9,10},{10,11},{12,13},{... | collective-permute-start | bytes 32648 | tf_op jit(solution)/shard_map/ppermute | solution.py:14
  161.8 1.5 copy.138
  163.3 2.6 %copy.140 = f32[8,10,34,1]{3,0,2,1:T(8,128)} copy(f32[8,10,34,1]{2,0,3,1:T(8,128)} %collective-permute-done.11) | data formatting | bytes 21760 | tf_op jit(solution)/shard_map/ppermute | solution.py:14
  165.8 3.0 %fusion.16 = f32[8,8,32,128]{3,0,2,1:T(8,128)S(1)} fusion(f32[8,10,34,1]{3,0,2,1:T(8,128)} %copy.140, f32[8,10,1,128]{3,0,2,1:T(8,128)S(1)} %collective-permute-done.8, f32[8,10,1,128]{3,0,2,1:T(8,128)} %copy-done.5, f32[8,1,32,128]{3,0,2,1:T(8,128)} %copy-done.1, f32[8,8,32,128]{3,0,2,1:T(8,128)S(1)} %bitcast.77, f32[8,1,32,128]{3,0,2,1:T(8,128)} %copy-done.2, ...), kind=kLoop, calls=%fused_computation.26 | loop fusion | flops 6553600 | bytes 2594048 | tf_op jit(solution)/shard_map/sub | solution.py:27
  168.9 3.0 %fusion = f32[24,8]{0,1:T(8,128)S(1)} fusion(f32[8,32768]{1,0:T(8,128)S(1)} %bitcast.82, f32[8,32768]{1,0:T(8,128)S(1)} %fusion.60, f32[8,32768]{1,0:T(8,128)S(1)} %fusion.12), kind=kOutput, calls=%fused_computation.1 | convolution fusion | flops 77070336 | bytes 3146496 | tf_op jit(solution)/shard_map/dot_general | solution.py:36
  171.9 42.0 %psum.23 = f32[24,8]{0,1:T(8,128)S(1)} all-reduce(f32[24,8]{0,1:T(8,128)S(1)} %fusion), channel_id=1, replica_groups=mesh['gx'=4,'gy'=2,'gz'=4] {'gx','gy','gz'}, use_global_device_ids=true, to_apply=%region_5.0 | all-reduce | flops 192 | bytes 1536 | tf_op jit(solution)/shard_map/psum | solution.py:51
  214.0 0.7 cholesky.116
  216.1 2.0 dynamic-slice_select_fusion
  218.1 1.7 scatter.20
  220.6 1.5 cholesky.41
  223.4 1.2 custom-call.15
  225.3 1.1 fusion.7
  227.0 1.2 copy.144
  (67 shorter events, 13.4 us)
Async XLA Ops:
  0.6 49.8 %copy-start = (f32[8,8,32,128]{3,2,1,0:T(8,128)S(1)}, f32[8,8,32,128]{3,2,1,0:T(8,128)}, u32[]{:S(2)}) copy-start(f32[8,8,32,128]{3,2,1,0:T(8,128)} %param.15) | copy-start | bytes 3145732
  51.9 7.1 %collective-permute-start = (f32[8,1,32,128]{3,0,2,1:T(8,128)S(1)}, f32[8,1,32,128]{3,0,2,1:T(8,128)S(1)}, u32[]{:S(2)}, u32[]{:S(2)}) collective-permute-start(f32[8,1,32,128]{3,0,2,1:T(8,128)S(1)} %get-tuple-element.85), channel_id=1, source_target_pairs={{8,0},{16,8},{24,16},{9,1},{17,9},{25,17},{10,2},{18,10},{26,18},{... | collective-permute-start | bytes 393224 | tf_op jit(solution)/shard_map/ppermute | solution.py:17
  53.2 7.3 %collective-permute-start.1 = (f32[8,1,32,128]{3,0,2,1:T(8,128)S(1)}, f32[8,1,32,128]{3,0,2,1:T(8,128)S(1)}, u32[]{:S(2)}, u32[]{:S(2)}) collective-permute-start(f32[8,1,32,128]{3,0,2,1:T(8,128)S(1)} %get-tuple-element.84), channel_id=1, source_target_pairs={{0,8},{8,16},{16,24},{1,9},{9,17},{17,25},{2,10},{10,18},{18,26},{... | collective-permute-start | bytes 393224 | tf_op jit(solution)/shard_map/ppermute | solution.py:14
  59.1 6.8 %copy-start.3 = (f32[8,1,32,128]{3,0,2,1:T(8,128)}, f32[8,1,32,128]{3,0,2,1:T(8,128)S(1)}, u32[]{:S(2)}) copy-start(f32[8,1,32,128]{3,0,2,1:T(8,128)S(1)} %collective-permute-done) | copy-start | bytes 393220
  60.6 5.3 %copy-start.4 = (f32[8,1,32,128]{3,0,2,1:T(8,128)}, f32[8,1,32,128]{3,0,2,1:T(8,128)S(1)}, u32[]{:S(2)}) copy-start(f32[8,1,32,128]{3,0,2,1:T(8,128)S(1)} %collective-permute-done.1) | copy-start | bytes 393220
  60.6 4.3 %collective-permute-start.2 = (f32[8,10,1,128]{3,0,2,1:T(8,128)S(1)}, f32[8,10,1,128]{3,0,2,1:T(8,128)S(1)}, u32[]{:S(2)}, u32[]{:S(2)}) collective-permute-start(f32[8,10,1,128]{3,0,2,1:T(8,128)S(1)} %get-tuple-element.81), channel_id=1, source_target_pairs={{4,0},{5,1},{6,2},{7,3},{12,8},{13,9},{14,10},{15,11},{20,16},{21,... | collective-permute-start | bytes 122888 | tf_op jit(solution)/shard_map/ppermute | solution.py:17
  61.9 3.9 %collective-permute-start.3 = (f32[8,10,1,128]{3,0,2,1:T(8,128)S(1)}, f32[8,10,1,128]{3,0,2,1:T(8,128)S(1)}, u32[]{:S(2)}, u32[]{:S(2)}) collective-permute-start(f32[8,10,1,128]{3,0,2,1:T(8,128)S(1)} %get-tuple-element.80), channel_id=1, source_target_pairs={{0,4},{1,5},{2,6},{3,7},{8,12},{9,13},{10,14},{11,15},{16,20},{17,... | collective-permute-start | bytes 122888 | tf_op jit(solution)/shard_map/ppermute | solution.py:14
  65.8 0.6 copy-start.6
  67.9 8.5 %copy-start.7 = (f32[8,32,128]{2,1,0:T(8,128)S(1)}, f32[8,32,128]{2,1,0:T(8,128)}, u32[]{:S(2)}) copy-start(f32[8,32,128]{2,1,0:T(8,128)} %param.16) | copy-start | bytes 393220
  70.0 7.2 %collective-permute-start.4 = (f32[8,10,34,1]{2,0,3,1:T(8,128)S(1)}, f32[8,10,34,1]{2,0,3,1:T(8,128)S(1)}, u32[]{:S(2)}, u32[]{:S(2)}) collective-permute-start(f32[8,10,34,1]{2,0,3,1:T(8,128)S(1)} %copy.130), channel_id=1, source_target_pairs={{1,0},{2,1},{3,2},{5,4},{6,5},{7,6},{9,8},{10,9},{11,10},{13,12},{... | collective-permute-start | bytes 32648 | tf_op jit(solution)/shard_map/ppermute | solution.py:17
  71.9 6.2 %collective-permute-start.5 = (f32[8,10,34,1]{2,0,3,1:T(8,128)S(1)}, f32[8,10,34,1]{2,0,3,1:T(8,128)S(1)}, u32[]{:S(2)}, u32[]{:S(2)}) collective-permute-start(f32[8,10,34,1]{2,0,3,1:T(8,128)S(1)} %copy.132), channel_id=1, source_target_pairs={{0,1},{1,2},{2,3},{4,5},{5,6},{6,7},{8,9},{9,10},{10,11},{12,13},{... | collective-permute-start | bytes 32648 | tf_op jit(solution)/shard_map/ppermute | solution.py:14
  133.7 7.3 %collective-permute-start.6 = (f32[8,1,32,128]{3,0,2,1:T(8,128)S(1)}, f32[8,1,32,128]{3,0,2,1:T(8,128)S(1)}, u32[]{:S(2)}, u32[]{:S(2)}) collective-permute-start(f32[8,1,32,128]{3,0,2,1:T(8,128)S(1)} %get-tuple-element.83), channel_id=1, source_target_pairs={{8,0},{16,8},{24,16},{9,1},{17,9},{25,17},{10,2},{18,10},{26,18},{... | collective-permute-start | bytes 393224 | tf_op jit(solution)/shard_map/ppermute | solution.py:17
  135.0 7.3 %collective-permute-start.7 = (f32[8,1,32,128]{3,0,2,1:T(8,128)S(1)}, f32[8,1,32,128]{3,0,2,1:T(8,128)S(1)}, u32[]{:S(2)}, u32[]{:S(2)}) collective-permute-start(f32[8,1,32,128]{3,0,2,1:T(8,128)S(1)} %get-tuple-element.82), channel_id=1, source_target_pairs={{0,8},{8,16},{16,24},{1,9},{9,17},{17,25},{2,10},{10,18},{18,26},{... | collective-permute-start | bytes 393224 | tf_op jit(solution)/shard_map/ppermute | solution.py:14
  141.1 6.5 %copy-start.1 = (f32[8,1,32,128]{3,0,2,1:T(8,128)}, f32[8,1,32,128]{3,0,2,1:T(8,128)S(1)}, u32[]{:S(2)}) copy-start(f32[8,1,32,128]{3,0,2,1:T(8,128)S(1)} %collective-permute-done.6) | copy-start | bytes 393220
  142.4 5.2 %copy-start.2 = (f32[8,1,32,128]{3,0,2,1:T(8,128)}, f32[8,1,32,128]{3,0,2,1:T(8,128)S(1)}, u32[]{:S(2)}) copy-start(f32[8,1,32,128]{3,0,2,1:T(8,128)S(1)} %collective-permute-done.7) | copy-start | bytes 393220
  142.4 4.4 %collective-permute-start.8 = (f32[8,10,1,128]{3,0,2,1:T(8,128)S(1)}, f32[8,10,1,128]{3,0,2,1:T(8,128)S(1)}, u32[]{:S(2)}, u32[]{:S(2)}) collective-permute-start(f32[8,10,1,128]{3,0,2,1:T(8,128)S(1)} %get-tuple-element.79), channel_id=1, source_target_pairs={{4,0},{5,1},{6,2},{7,3},{12,8},{13,9},{14,10},{15,11},{20,16},{21,... | collective-permute-start | bytes 122888 | tf_op jit(solution)/shard_map/ppermute | solution.py:17
  143.7 3.9 %collective-permute-start.9 = (f32[8,10,1,128]{3,0,2,1:T(8,128)S(1)}, f32[8,10,1,128]{3,0,2,1:T(8,128)S(1)}, u32[]{:S(2)}, u32[]{:S(2)}) collective-permute-start(f32[8,10,1,128]{3,0,2,1:T(8,128)S(1)} %get-tuple-element.78), channel_id=1, source_target_pairs={{0,4},{1,5},{2,6},{3,7},{8,12},{9,13},{10,14},{11,15},{16,20},{17,... | collective-permute-start | bytes 122888 | tf_op jit(solution)/shard_map/ppermute | solution.py:14
  147.6 0.6 copy-start.5
  152.4 9.4 %collective-permute-start.10 = (f32[8,10,34,1]{2,0,3,1:T(8,128)}, f32[8,10,34,1]{2,0,3,1:T(8,128)}, u32[]{:S(2)}, u32[]{:S(2)}) collective-permute-start(f32[8,10,34,1]{2,0,3,1:T(8,128)} %copy.137), channel_id=1, source_target_pairs={{1,0},{2,1},{3,2},{5,4},{6,5},{7,6},{9,8},{10,9},{11,10},{13,12},{... | collective-permute-start | bytes 32648 | tf_op jit(solution)/shard_map/ppermute | solution.py:17
  155.0 8.3 %collective-permute-start.11 = (f32[8,10,34,1]{2,0,3,1:T(8,128)}, f32[8,10,34,1]{2,0,3,1:T(8,128)}, u32[]{:S(2)}, u32[]{:S(2)}) collective-permute-start(f32[8,10,34,1]{2,0,3,1:T(8,128)} %copy.139), channel_id=1, source_target_pairs={{0,1},{1,2},{2,3},{4,5},{5,6},{6,7},{8,9},{9,10},{10,11},{12,13},{... | collective-permute-start | bytes 32648 | tf_op jit(solution)/shard_map/ppermute | solution.py:14
where the time goes:
time: 229 us; the launch traced here: 228 us
  blocking collectives  127 us (55%)
  starting transfers between devices  33.1 us (14%)
  local copies, waits for them, and re-layouts  22.6 us (10%)
  other arithmetic  21 us (9%)
  matrix products  16.4 us (7%)
  waiting for transfers between devices  6.95 us (3%)
    psum x2, blocking collectives, body(): lax.psum(small_dot(jnp.concatenate([stacked, image], axis=0), image.T), (...  85.1 us
    psum x1, blocking collectives, body(): gram = lax.psum(small_dot(rows, rows.T), ('gx', 'gy', 'gz'))  42 us
    ppermute x6, starting transfers between devices, padded_2(): lax.ppermute(lax.slice_in_dim(block, block.shape[dim] - width, None, axis...  25.4 us
    dot_general x12, matrix products, small_dot(): return jnp.dot(left, right, precision=lax.Precision.HIGHEST)  15.7 us
    ppermute x6, starting transfers between devices, padded_2(): lax.ppermute(lax.slice_in_dim(block, 0, width, axis=dim), axis, backward)  7.73 us
    slice x4, local copies, waits for them, and re-layouts, padded_2(): lax.slice_in_dim(block, 0, width, axis=dim)  7.72 us
    sub x2, other arithmetic, operate(): return (6.0 + shift)[None] * fields - beside  6.01 us
    ppermute x6, waiting for transfers between devices, padded_2(): lax.ppermute(lax.slice_in_dim(block, block.shape[dim] - width, None, axis...  4.75 us
  transfers between devices with their start and end apart: 12, of which 7 were waited for; matrix products, arithmetic and copies ran while one was open for 3% of the time, Pallas kernels for 0%

commit v1 on v0

--- a/solution.py
+++ b/solution.py
@@ -40,7 +40,7 @@
     width = right_side.shape[0]
     shape = right_side.shape
     rows = right_side.reshape(width, -1)
-    gram = lax.psum(small_dot(rows, rows.T), ("gx", "gy", "gz"))
+    gram = lax.psum(lax.psum(small_dot(rows, rows.T), axis_name="gx"), ("gy", "gz"))
     lower = jnp.linalg.cholesky(gram)
     start_coeff = lower.T
     basis = [small_dot(lower_inverse(lower), rows)]

time: 229 us -> 211 us (0.921)
  blocking collectives: 127 us -> 109 us
    psum x1 -> x2, blocking collectives: 42 us -> 26.8 us  [the longest x1 15.4 us: body(): lax.psum(lax.psum(small_dot(rows, rows.T), axis_name='gx'), ('gy', 'gz'))]
    psum x2, blocking collectives: 85.1 us -> 82.6 us  [body(): lax.psum(small_dot(jnp.concatenate([stacked, image], axis=0), image.T), (...]
where the time goes in v1:
time: 211 us; the launch traced here: 210 us
  blocking collectives  109 us (52%)
  starting transfers between devices  32.9 us (16%)
  local copies, waits for them, and re-layouts  22.1 us (10%)
  other arithmetic  21 us (10%)
  matrix products  16.4 us (8%)
  waiting for transfers between devices  7.56 us (4%)
    psum x2, blocking collectives, body(): lax.psum(small_dot(jnp.concatenate([stacked, image], axis=0), image.T), (...  82.6 us
    ppermute x6, starting transfers between devices, padded_2(): lax.ppermute(lax.slice_in_dim(block, block.shape[dim] - width, None, axis...  25.1 us
    dot_general x12, matrix products, small_dot(): return jnp.dot(left, right, precision=lax.Precision.HIGHEST)  15.7 us
    psum x1, blocking collectives, body(): lax.psum(lax.psum(small_dot(rows, rows.T), axis_name='gx'), ('gy', 'gz'))  15.4 us
    psum x1, blocking collectives, body(): lax.psum(small_dot(rows, rows.T), axis_name='gx')  11.4 us
    ppermute x6, starting transfers between devices, padded_2(): lax.ppermute(lax.slice_in_dim(block, 0, width, axis=dim), axis, backward)  7.73 us
    slice x4, local copies, waits for them, and re-layouts, padded_2(): lax.slice_in_dim(block, 0, width, axis=dim)  7.72 us
    sub x2, other arithmetic, operate(): return (6.0 + shift)[None] * fields - beside  6.01 us
  transfers between devices with their start and end apart: 12, of which 7 were waited for; matrix products, arithmetic and copies ran while one was open for 3% of the time, Pallas kernels for 0%

profile of v1, /device:TPU:0, one launch (start us, length us, event | category | flops | bytes accessed | tf_op | source)
XLA Modules:
  0.0 210.3 jit_solution(2657746348880306665)
XLA Ops:
  0.6 4.9 %convolution_bitcast_fusion = f32[8,8]{0,1:T(8,128)S(1)} fusion(f32[8,8,32,128]{3,2,1,0:T(8,128)} %param.15), kind=kOutput, calls=%fused_computation.19 | convolution fusion | flops 25165824 | bytes 1048832 | tf_op jit(solution)/shard_map/dot_general | solution.py:36
  5.5 11.4 %psum.28 = f32[8,8]{0,1:T(8,128)S(1)} all-reduce(f32[8,8]{0,1:T(8,128)S(1)} %convolution_bitcast_fusion), channel_id=1, replica_groups=mesh['gx'=4,'gy'=2,'gz'=4] {'gx'}, use_global_device_ids=true, to_apply=%region_0.0 | all-reduce | flops 64 | bytes 512 | tf_op jit(solution)/shard_map/psum | solution.py:43
  16.9 15.4 %psum.29 = f32[8,8]{0,1:T(8,128)S(1)} all-reduce(f32[8,8]{0,1:T(8,128)S(1)} %psum.28), channel_id=1, replica_groups=mesh['gx'=4,'gy'=2,'gz'=4] {'gy','gz'}, use_global_device_ids=true, to_apply=%region_1.0 | all-reduce | flops 64 | bytes 512 | tf_op jit(solution)/shard_map/psum | solution.py:43
  32.4 0.7 cholesky.94
  35.2 1.5 fusion.12
  36.8 1.3 collective-permute-start
  38.1 4.6 %collective-permute-start.1 = (f32[8,1,32,128]{3,0,2,1:T(8,128)S(1)}, f32[8,1,32,128]{3,0,2,1:T(8,128)S(1)}, u32[]{:S(2)}, u32[]{:S(2)}) collective-permute-start(f32[8,1,32,128]{3,0,2,1:T(8,128)S(1)} %get-tuple-element.84), channel_id=1, source_target_pairs={{0,8},{8,16},{16,24},{1,9},{9,17},{17,25},{2,10},{10,18},{18,26},{... | collective-permute-start | bytes 393224 | tf_op jit(solution)/shard_map/ppermute | solution.py:14
  42.6 1.4 collective-permute-done
  44.0 1.7 collective-permute-done.1
  45.7 1.3 collective-permute-start.2
  47.0 3.0 %collective-permute-start.3 = (f32[8,10,1,128]{3,0,2,1:T(8,128)S(1)}, f32[8,10,1,128]{3,0,2,1:T(8,128)S(1)}, u32[]{:S(2)}, u32[]{:S(2)}) collective-permute-start(f32[8,10,1,128]{3,0,2,1:T(8,128)S(1)} %get-tuple-element.80), channel_id=1, source_target_pairs={{0,4},{1,5},{2,6},{3,7},{8,12},{9,13},{10,14},{11,15},{16,20},{17,... | collective-permute-start | bytes 122888 | tf_op jit(solution)/shard_map/ppermute | solution.py:14
  50.1 0.8 collective-permute-done.3
  51.1 1.5 fusion.56
  52.6 2.0 copy.130
  54.6 1.3 collective-permute-start.4
  56.6 4.5 %collective-permute-start.5 = (f32[8,10,34,1]{2,0,3,1:T(8,128)S(1)}, f32[8,10,34,1]{2,0,3,1:T(8,128)S(1)}, u32[]{:S(2)}, u32[]{:S(2)}) collective-permute-start(f32[8,10,34,1]{2,0,3,1:T(8,128)S(1)} %copy.132), channel_id=1, source_target_pairs={{0,1},{1,2},{2,3},{4,5},{5,6},{6,7},{8,9},{9,10},{10,11},{12,13},{... | collective-permute-start | bytes 32648 | tf_op jit(solution)/shard_map/ppermute | solution.py:14
  61.8 0.7 copy.131
  62.8 1.8 copy.133
  64.6 3.0 %fusion.22 = f32[8,8,32,128]{3,0,2,1:T(8,128)S(1)} fusion(f32[8,10,34,1]{3,0,2,1:T(8,128)} %copy.133, f32[8,10,1,128]{3,0,2,1:T(8,128)S(1)} %collective-permute-done.2, f32[8,10,1,128]{3,0,2,1:T(8,128)} %copy-done.6, f32[8,1,32,128]{3,0,2,1:T(8,128)} %copy-done.3, f32[8,8,32,128]{3,0,2,1:T(8,128)S(1)} %bitcast.73, f32[8,1,32,128]{3,0,2,1:T(8,128)} %copy-done.4, ...), kind=kLoop, calls=%fused_computation.50 | loop fusion | flops 6553600 | bytes 2594048 | tf_op jit(solution)/shard_map/sub | solution.py:27
  67.6 2.6 %fusion.6 = f32[16,8]{0,1:T(8,128)S(1)} fusion(f32[8,32768]{1,0:T(8,128)S(1)} %bitcast.78, f32[8,32768]{1,0:T(8,128)S(1)} %fusion.12), kind=kOutput, calls=%fused_computation.9 | convolution fusion | flops 50855936 | bytes 2097664 | tf_op jit(solution)/shard_map/dot_general | solution.py:36
  70.1 41.3 %psum.30 = f32[16,8]{0,1:T(8,128)S(1)} all-reduce(f32[16,8]{0,1:T(8,128)S(1)} %fusion.6), channel_id=1, replica_groups=mesh['gx'=4,'gy'=2,'gz'=4] {'gx','gy','gz'}, use_global_device_ids=true, to_apply=%region_4.0 | all-reduce | flops 128 | bytes 1024 | tf_op jit(solution)/shard_map/psum | solution.py:51
  111.5 1.0 convolution_subtract_fusion
  112.6 0.7 cholesky.105
  115.5 1.0 fusion.60
  116.6 1.3 collective-permute-start.6
  117.9 4.8 %collective-permute-start.7 = (f32[8,1,32,128]{3,0,2,1:T(8,128)S(1)}, f32[8,1,32,128]{3,0,2,1:T(8,128)S(1)}, u32[]{:S(2)}, u32[]{:S(2)}) collective-permute-start(f32[8,1,32,128]{3,0,2,1:T(8,128)S(1)} %get-tuple-element.82), channel_id=1, source_target_pairs={{0,8},{8,16},{16,24},{1,9},{9,17},{17,25},{2,10},{10,18},{18,26},{... | collective-permute-start | bytes 393224 | tf_op jit(solution)/shard_map/ppermute | solution.py:14
  122.7 1.3 collective-permute-done.6
  124.0 1.2 collective-permute-done.7
  125.2 1.3 collective-permute-start.8
  126.5 3.0 %collective-permute-start.9 = (f32[8,10,1,128]{3,0,2,1:T(8,128)S(1)}, f32[8,10,1,128]{3,0,2,1:T(8,128)S(1)}, u32[]{:S(2)}, u32[]{:S(2)}) collective-permute-start(f32[8,10,1,128]{3,0,2,1:T(8,128)S(1)} %get-tuple-element.78), channel_id=1, source_target_pairs={{0,4},{1,5},{2,6},{3,7},{8,12},{9,13},{10,14},{11,15},{16,20},{17,... | collective-permute-start | bytes 122888 | tf_op jit(solution)/shard_map/ppermute | solution.py:14
  129.6 0.8 collective-permute-done.9
  131.1 1.5 fusion.55
  132.6 2.6 %copy.137 = f32[8,10,34,1]{2,0,3,1:T(8,128)} copy(f32[8,10,34,1]{3,0,2,1:T(8,128)} %get-tuple-element.74) | data formatting | bytes 21760 | tf_op jit(solution)/shard_map/slice | solution.py:17
  135.3 1.3 collective-permute-start.10
  136.5 1.3 copy.139
  137.8 5.2 %collective-permute-start.11 = (f32[8,10,34,1]{2,0,3,1:T(8,128)}, f32[8,10,34,1]{2,0,3,1:T(8,128)}, u32[]{:S(2)}, u32[]{:S(2)}) collective-permute-start(f32[8,10,34,1]{2,0,3,1:T(8,128)} %copy.139), channel_id=1, source_target_pairs={{0,1},{1,2},{2,3},{4,5},{5,6},{6,7},{8,9},{9,10},{10,11},{12,13},{... | collective-permute-start | bytes 32648 | tf_op jit(solution)/shard_map/ppermute | solution.py:14
  144.7 1.5 copy.138
  146.1 2.6 %copy.140 = f32[8,10,34,1]{3,0,2,1:T(8,128)} copy(f32[8,10,34,1]{2,0,3,1:T(8,128)} %collective-permute-done.11) | data formatting | bytes 21760 | tf_op jit(solution)/shard_map/ppermute | solution.py:14
  148.7 3.0 %fusion.16 = f32[8,8,32,128]{3,0,2,1:T(8,128)S(1)} fusion(f32[8,10,34,1]{3,0,2,1:T(8,128)} %copy.140, f32[8,10,1,128]{3,0,2,1:T(8,128)S(1)} %collective-permute-done.8, f32[8,10,1,128]{3,0,2,1:T(8,128)} %copy-done.5, f32[8,1,32,128]{3,0,2,1:T(8,128)} %copy-done.1, f32[8,8,32,128]{3,0,2,1:T(8,128)S(1)} %bitcast.77, f32[8,1,32,128]{3,0,2,1:T(8,128)} %copy-done.2, ...), kind=kLoop, calls=%fused_computation.26 | loop fusion | flops 6553600 | bytes 2594048 | tf_op jit(solution)/shard_map/sub | solution.py:27
  151.7 3.0 %fusion = f32[24,8]{0,1:T(8,128)S(1)} fusion(f32[8,32768]{1,0:T(8,128)S(1)} %bitcast.82, f32[8,32768]{1,0:T(8,128)S(1)} %fusion.60, f32[8,32768]{1,0:T(8,128)S(1)} %fusion.12), kind=kOutput, calls=%fused_computation.1 | convolution fusion | flops 77070336 | bytes 3146496 | tf_op jit(solution)/shard_map/dot_general | solution.py:36
  154.7 41.3 %psum.31 = f32[24,8]{0,1:T(8,128)S(1)} all-reduce(f32[24,8]{0,1:T(8,128)S(1)} %fusion), channel_id=1, replica_groups=mesh['gx'=4,'gy'=2,'gz'=4] {'gx','gy','gz'}, use_global_device_ids=true, to_apply=%region_6.0 | all-reduce | flops 192 | bytes 1536 | tf_op jit(solution)/shard_map/psum | solution.py:51
  196.2 0.7 cholesky.116
  198.3 2.0 dynamic-slice_select_fusion
  200.3 1.7 scatter.20
  202.8 1.5 cholesky.41
  205.6 1.2 custom-call.15
  207.5 1.1 fusion.7
  209.1 1.2 copy.144
  (68 shorter events, 13.5 us)
Async XLA Ops:
  0.6 34.6 %copy-start = (f32[8,8,32,128]{3,2,1,0:T(8,128)S(1)}, f32[8,8,32,128]{3,2,1,0:T(8,128)}, u32[]{:S(2)}) copy-start(f32[8,8,32,128]{3,2,1,0:T(8,128)} %param.15) | copy-start | bytes 3145732
  36.8 7.2 %collective-permute-start = (f32[8,1,32,128]{3,0,2,1:T(8,128)S(1)}, f32[8,1,32,128]{3,0,2,1:T(8,128)S(1)}, u32[]{:S(2)}, u32[]{:S(2)}) collective-permute-start(f32[8,1,32,128]{3,0,2,1:T(8,128)S(1)} %get-tuple-element.85), channel_id=1, source_target_pairs={{8,0},{16,8},{24,16},{9,1},{17,9},{25,17},{10,2},{18,10},{26,18},{... | collective-permute-start | bytes 393224 | tf_op jit(solution)/shard_map/ppermute | solution.py:17
  38.1 7.7 %collective-permute-start.1 = (f32[8,1,32,128]{3,0,2,1:T(8,128)S(1)}, f32[8,1,32,128]{3,0,2,1:T(8,128)S(1)}, u32[]{:S(2)}, u32[]{:S(2)}) collective-permute-start(f32[8,1,32,128]{3,0,2,1:T(8,128)S(1)} %get-tuple-element.84), channel_id=1, source_target_pairs={{0,8},{8,16},{16,24},{1,9},{9,17},{17,25},{2,10},{10,18},{18,26},{... | collective-permute-start | bytes 393224 | tf_op jit(solution)/shard_map/ppermute | solution.py:14
  44.0 7.0 %copy-start.3 = (f32[8,1,32,128]{3,0,2,1:T(8,128)}, f32[8,1,32,128]{3,0,2,1:T(8,128)S(1)}, u32[]{:S(2)}) copy-start(f32[8,1,32,128]{3,0,2,1:T(8,128)S(1)} %collective-permute-done) | copy-start | bytes 393220
  45.7 5.3 %copy-start.4 = (f32[8,1,32,128]{3,0,2,1:T(8,128)}, f32[8,1,32,128]{3,0,2,1:T(8,128)S(1)}, u32[]{:S(2)}) copy-start(f32[8,1,32,128]{3,0,2,1:T(8,128)S(1)} %collective-permute-done.1) | copy-start | bytes 393220
  45.7 4.3 %collective-permute-start.2 = (f32[8,10,1,128]{3,0,2,1:T(8,128)S(1)}, f32[8,10,1,128]{3,0,2,1:T(8,128)S(1)}, u32[]{:S(2)}, u32[]{:S(2)}) collective-permute-start(f32[8,10,1,128]{3,0,2,1:T(8,128)S(1)} %get-tuple-element.81), channel_id=1, source_target_pairs={{4,0},{5,1},{6,2},{7,3},{12,8},{13,9},{14,10},{15,11},{20,16},{21,... | collective-permute-start | bytes 122888 | tf_op jit(solution)/shard_map/ppermute | solution.py:17
  47.0 3.9 %collective-permute-start.3 = (f32[8,10,1,128]{3,0,2,1:T(8,128)S(1)}, f32[8,10,1,128]{3,0,2,1:T(8,128)S(1)}, u32[]{:S(2)}, u32[]{:S(2)}) collective-permute-start(f32[8,10,1,128]{3,0,2,1:T(8,128)S(1)} %get-tuple-element.80), channel_id=1, source_target_pairs={{0,4},{1,5},{2,6},{3,7},{8,12},{9,13},{10,14},{11,15},{16,20},{17,... | collective-permute-start | bytes 122888 | tf_op jit(solution)/shard_map/ppermute | solution.py:14
  50.9 1.7 copy-start.6
  52.6 8.5 %copy-start.7 = (f32[8,32,128]{2,1,0:T(8,128)S(1)}, f32[8,32,128]{2,1,0:T(8,128)}, u32[]{:S(2)}) copy-start(f32[8,32,128]{2,1,0:T(8,128)} %param.16) | copy-start | bytes 393220
  54.6 7.2 %collective-permute-start.4 = (f32[8,10,34,1]{2,0,3,1:T(8,128)S(1)}, f32[8,10,34,1]{2,0,3,1:T(8,128)S(1)}, u32[]{:S(2)}, u32[]{:S(2)}) collective-permute-start(f32[8,10,34,1]{2,0,3,1:T(8,128)S(1)} %copy.130), channel_id=1, source_target_pairs={{1,0},{2,1},{3,2},{5,4},{6,5},{7,6},{9,8},{10,9},{11,10},{13,12},{... | collective-permute-start | bytes 32648 | tf_op jit(solution)/shard_map/ppermute | solution.py:17
  56.6 6.2 %collective-permute-start.5 = (f32[8,10,34,1]{2,0,3,1:T(8,128)S(1)}, f32[8,10,34,1]{2,0,3,1:T(8,128)S(1)}, u32[]{:S(2)}, u32[]{:S(2)}) collective-permute-start(f32[8,10,34,1]{2,0,3,1:T(8,128)S(1)} %copy.132), channel_id=1, source_target_pairs={{0,1},{1,2},{2,3},{4,5},{5,6},{6,7},{8,9},{9,10},{10,11},{12,13},{... | collective-permute-start | bytes 32648 | tf_op jit(solution)/shard_map/ppermute | solution.py:14
  116.6 7.4 %collective-permute-start.6 = (f32[8,1,32,128]{3,0,2,1:T(8,128)S(1)}, f32[8,1,32,128]{3,0,2,1:T(8,128)S(1)}, u32[]{:S(2)}, u32[]{:S(2)}) collective-permute-start(f32[8,1,32,128]{3,0,2,1:T(8,128)S(1)} %get-tuple-element.83), channel_id=1, source_target_pairs={{8,0},{16,8},{24,16},{9,1},{17,9},{25,17},{10,2},{18,10},{26,18},{... | collective-permute-start | bytes 393224 | tf_op jit(solution)/shard_map/ppermute | solution.py:17
  117.9 7.3 %collective-permute-start.7 = (f32[8,1,32,128]{3,0,2,1:T(8,128)S(1)}, f32[8,1,32,128]{3,0,2,1:T(8,128)S(1)}, u32[]{:S(2)}, u32[]{:S(2)}) collective-permute-start(f32[8,1,32,128]{3,0,2,1:T(8,128)S(1)} %get-tuple-element.82), channel_id=1, source_target_pairs={{0,8},{8,16},{16,24},{1,9},{9,17},{17,25},{2,10},{10,18},{18,26},{... | collective-permute-start | bytes 393224 | tf_op jit(solution)/shard_map/ppermute | solution.py:14
  124.0 6.4 %copy-start.1 = (f32[8,1,32,128]{3,0,2,1:T(8,128)}, f32[8,1,32,128]{3,0,2,1:T(8,128)S(1)}, u32[]{:S(2)}) copy-start(f32[8,1,32,128]{3,0,2,1:T(8,128)S(1)} %collective-permute-done.6) | copy-start | bytes 393220
  125.2 5.2 %copy-start.2 = (f32[8,1,32,128]{3,0,2,1:T(8,128)}, f32[8,1,32,128]{3,0,2,1:T(8,128)S(1)}, u32[]{:S(2)}) copy-start(f32[8,1,32,128]{3,0,2,1:T(8,128)S(1)} %collective-permute-done.7) | copy-start | bytes 393220
  125.2 4.4 %collective-permute-start.8 = (f32[8,10,1,128]{3,0,2,1:T(8,128)S(1)}, f32[8,10,1,128]{3,0,2,1:T(8,128)S(1)}, u32[]{:S(2)}, u32[]{:S(2)}) collective-permute-start(f32[8,10,1,128]{3,0,2,1:T(8,128)S(1)} %get-tuple-element.79), channel_id=1, source_target_pairs={{4,0},{5,1},{6,2},{7,3},{12,8},{13,9},{14,10},{15,11},{20,16},{21,... | collective-permute-start | bytes 122888 | tf_op jit(solution)/shard_map/ppermute | solution.py:17
  126.5 3.9 %collective-permute-start.9 = (f32[8,10,1,128]{3,0,2,1:T(8,128)S(1)}, f32[8,10,1,128]{3,0,2,1:T(8,128)S(1)}, u32[]{:S(2)}, u32[]{:S(2)}) collective-permute-start(f32[8,10,1,128]{3,0,2,1:T(8,128)S(1)} %get-tuple-element.78), channel_id=1, source_target_pairs={{0,4},{1,5},{2,6},{3,7},{8,12},{9,13},{10,14},{11,15},{16,20},{17,... | collective-permute-start | bytes 122888 | tf_op jit(solution)/shard_map/ppermute | solution.py:14
  130.4 0.6 copy-start.5
  135.3 9.4 %collective-permute-start.10 = (f32[8,10,34,1]{2,0,3,1:T(8,128)}, f32[8,10,34,1]{2,0,3,1:T(8,128)}, u32[]{:S(2)}, u32[]{:S(2)}) collective-permute-start(f32[8,10,34,1]{2,0,3,1:T(8,128)} %copy.137), channel_id=1, source_target_pairs={{1,0},{2,1},{3,2},{5,4},{6,5},{7,6},{9,8},{10,9},{11,10},{13,12},{... | collective-permute-start | bytes 32648 | tf_op jit(solution)/shard_map/ppermute | solution.py:17
  137.8 8.3 %collective-permute-start.11 = (f32[8,10,34,1]{2,0,3,1:T(8,128)}, f32[8,10,34,1]{2,0,3,1:T(8,128)}, u32[]{:S(2)}, u32[]{:S(2)}) collective-permute-start(f32[8,10,34,1]{2,0,3,1:T(8,128)} %copy.139), channel_id=1, source_target_pairs={{0,1},{1,2},{2,3},{4,5},{5,6},{6,7},{8,9},{9,10},{10,11},{12,13},{... | collective-permute-start | bytes 32648 | tf_op jit(solution)/shard_map/ppermute | solution.py:14
